TPU v7x, 128 devices: a whole 4x4x4 slice. The times are simulated.
128 devices in a mesh: fsdp: 8 (over z_hi, y), tp: 16 (over z_lo, x, core).
Axes of the slice: x: 4, y: 4, z: 4 (z_hi: 2, z_lo: 2; z = z_hi * 2 + z_lo), core: 2. Of those that a mesh axis runs over, the one named last changes fastest.
Arguments:
- tokens: bfloat16 [2048, 8192], P('fsdp', 'tp'), may hold values from -6 to 6
- out_grad: bfloat16 [2048, 8192], P('fsdp', 'tp'), may hold values from -6 to 6
- gate_weight: bfloat16 [8192, 2048], P('fsdp', 'tp'), may hold values from -0.0625 to 0.0625
- up_weight: bfloat16 [8192, 2048], P('fsdp', 'tp'), may hold values from -0.0625 to 0.0625
- down_weight: bfloat16 [2048, 8192], P('tp', 'fsdp'), may hold values from -0.125 to 0.125
Outputs:
- input_grad: bfloat16 [2048, 8192], P('fsdp', 'tp')
- gate_grad: float32 [8192, 2048], P('fsdp', 'tp')
- up_grad: float32 [8192, 2048], P('fsdp', 'tp')
- down_grad: float32 [2048, 8192], P('tp', 'fsdp')
All inputs are finite; a program needn't handle non-finite values.
Results may differ from a plain program's by a relative error of at most 0.0023.
Values may be sent and summed in bfloat16 or wider, within the bound.
No kernel may reach another device: no remote copies, remote signals or barrier semaphores. Data moves between devices by JAX's collectives and lax.ppermute only.
A program may use at most 128 MiB of HBM per device.

v0:
```python
import math
import jax
import jax.numpy as jnp
from jax import lax
from jax.sharding import Mesh
from jax.sharding import PartitionSpec as P

FSDP = ("fsdp_0", "fsdp_1")


def laid_out(parts, dim):
    parts = jnp.moveaxis(parts, 0, dim)
    dims = parts.shape
    return parts.reshape(*dims[:dim], dims[dim] * dims[dim + 1], *dims[dim + 2 :])


def one_gather(arrays, axis, dims):
    line = jnp.concatenate([a.reshape(-1) for a in arrays])
    lines, at, outs = (lax.all_gather(line, axis), 0, [])
    for a, dim in zip(arrays, dims):
        parts = lines[:, at : at + a.size].reshape(-1, *a.shape)
        outs.append(laid_out(parts, dim))
        at += a.size
    return tuple(outs)


def stacked_from(value, axes, turns):
    parts = value[None]
    for k in turns:
        parts = lax.all_gather(parts, axes[k], axis=0, tiled=True)
    current = [lax.axis_size(axes[k]) for k in reversed(turns)]
    parts = parts.reshape(*current, *value.shape)
    turned = sorted(range(len(turns)), key=lambda place: turns[len(turns) - 1 - place])
    return parts.transpose(*turned, *range(len(turns), parts.ndim)).reshape(-1, *value.shape)


def gathered_by_axis(value, axes, turns, dim):
    return laid_out(stacked_from(value, axes, turns), dim)


def taken_in(value, axes, turns, dim, absorb, carry):
    everything = jax.tree.map(lambda part: gathered_by_axis(part, axes, turns, dim), value)
    return absorb(carry, everything, jnp.int32(0))


def own_rows(portion, rows, axis):
    count = rows * lax.axis_size(axis)
    return lax.psum_scatter(portion(jnp.int32(0), count), axis, scatter_dimension=0, tiled=True)


def column_term(left, right, start, count, factor):
    block = lax.dynamic_slice_in_dim(left, start, count, 1)
    product = lax.dot_general(
        block, right, (((0,), (0,)), ((), ())), preferred_element_type=jnp.float32
    )
    return product * factor


def shards(tokens, out_grad, gate_weight, up_weight, down_weight):
    factor = 1.0 / math.sqrt(tokens.shape[0] * lax.axis_size(FSDP))
    whole = lax.all_gather(tokens, "tp", axis=1, tiled=True)
    grads = lax.all_gather(out_grad, "tp", axis=1, tiled=True)
    gate_full, up_full = one_gather((gate_weight, up_weight), FSDP, (0, 0))
    gate = jnp.dot(whole, gate_full, preferred_element_type=jnp.float32)
    up = jnp.dot(whole, up_full, preferred_element_type=jnp.float32)

    def add_down(total, piece, start):
        columns = lax.dynamic_slice_in_dim(grads, start, piece.shape[1], 1)
        return total + lax.dot_general(
            columns, piece, (((1,), (1,)), ((), ())), preferred_element_type=jnp.float32
        )

    initial = jnp.zeros((whole.shape[0], down_weight.shape[0]), jnp.float32)
    hidden_grad = taken_in(down_weight, FSDP, (0, 1), 1, add_down, initial)
    squashed = jax.nn.sigmoid(gate)
    activated = gate * squashed
    slope = squashed * (1.0 + gate * (1.0 - squashed))
    hidden = (activated * up).astype(jnp.bfloat16)
    gate_delta = (hidden_grad * up * slope).astype(jnp.bfloat16)
    up_delta = (hidden_grad * activated).astype(jnp.bfloat16)

    def rows_term(start, count):
        gate_rows = lax.dynamic_slice_in_dim(gate_full, start, count, 0)
        up_rows = lax.dynamic_slice_in_dim(up_full, start, count, 0)
        first = lax.dot_general(
            gate_rows, gate_delta, (((1,), (1,)), ((), ())), preferred_element_type=jnp.float32
        )
        second = lax.dot_general(
            up_rows, up_delta, (((1,), (1,)), ((), ())), preferred_element_type=jnp.float32
        )
        return first + second

    local_rows = own_rows(rows_term, tokens.shape[1], "tp")
    input_grad = local_rows.T.astype(jnp.bfloat16)
    rows_here = gate_weight.shape[0]

    def joint_term(start, count):
        return jnp.concatenate(
            [
                column_term(whole, gate_delta, start, count, factor),
                column_term(whole, up_delta, start, count, factor),
                column_term(grads, hidden, start, count, factor),
            ],
            axis=1,
        )

    summed = own_rows(joint_term, rows_here, FSDP)
    width = gate_delta.shape[1]
    gate_grad = summed[:, :width]
    up_grad = summed[:, width : 2 * width]
    down_grad = summed[:, 2 * width :].T
    return (input_grad, gate_grad, up_grad, down_grad)


def solution(mesh):
    finer = Mesh(mesh.devices.reshape(2, 4, mesh.shape["tp"]), ("fsdp_0", "fsdp_1", "tp"))
    return jax.shard_map(
        shards,
        mesh=finer,
        in_specs=(P(FSDP, "tp"), P(FSDP, "tp"), P(FSDP, "tp"), P(FSDP, "tp"), P("tp", FSDP)),
        out_specs=(P(FSDP, "tp"), P(FSDP, "tp"), P(FSDP, "tp"), P("tp", FSDP)),
        check_vma=False,
    )
```

profile of v0, /device:TPU:0, one launch (start us, length us, event | category | flops | bytes accessed | tf_op | source)
XLA Modules:
  0.0 450.9 jit_solution(1478735136044264735)
XLA Ops:
  7.2 0.0 all-gather.9.cloned.1.call-start
  7.2 12.9 %all-gather.1 = bf16[256,1024]{1,0:T(8,128)(2,1)} all-gather(bf16[128,1024]{1,0:T(8,128)(2,1)} %param.9), channel_id=3, replica_groups=mesh['fsdp_0'=2,'fsdp_1'=4,'tp'=16] {'fsdp_0'}, dimensions={0}, use_global_device_ids=true | all-gather | bytes 786432 | tf_op jit(solution)/shard_map/all_gather | solution.py:30
  20.1 0.0 all-gather.9.cloned.1.call-update
  20.2 0.0 all-gather.13.cloned.1.call-start
  20.2 1.9 pad_maximum_fusion.1
  22.1 0.0 all-gather.13.cloned.1.call-update
  22.1 0.0 all-gather.11.cloned.1.call-start
  22.1 0.7 all-gather.11.cloned.1.call-update
  22.8 0.0 all-gather.7.cloned.1.call-start
  22.9 0.5 all-gather.7.cloned.1.call-update
  23.4 0.0 reduce-scatter.3.cloned.1.call-start
  23.5 27.7 %all-gather.9.cloned.1.call-done = bf16[8,128,1024]{2,1,0:T(8,128)(2,1)} async-done(((bf16[2,128,1024]{2,1,0:T(8,128)(2,1)}), bf16[8,128,1024]{2,1,0:T(8,128)(2,1)}) %all-gather.9.cloned.1.call-update) | async-done | bytes 2097168 | tf_op jit(solution)/shard_map/all_gather | solution.py:30
  51.2 1.9 copy.27
  53.1 2.4 copy.28
  55.5 70.3 %all-gather.13.cloned.1.call-done = bf16[2097152]{0:T(1024)(128)(2,1)} async-done(((bf16[262144]{0:T(1024)(128)(2,1)}), bf16[2097152]{0:T(1024)(128)(2,1)}) %all-gather.13.cloned.1.call-update) | async-done | bytes 4194320 | tf_op jit(solution)/shard_map/all_gather | solution.py:19
  125.8 5.9 %reshape.28 = bf16[8,262144]{1,0:T(8,128)(2,1)} reshape(bf16[2097152]{0:T(1024)(128)(2,1)} %all-gather.13.cloned.1.call-done) | data formatting | bytes 8388608 | tf_op jit(solution)/shard_map/all_gather | solution.py:19
  131.7 3.9 fusion.6
  135.6 2.3 reshape_reshape.6
  137.9 2.6 reshape_reshape.7
  140.4 21.9 %all-gather.11.cloned.1.call-done = bf16[256,8192]{1,0:T(8,128)(2,1)} async-done(((bf16[256,512]{1,0:T(8,128)(2,1)}), bf16[256,8192]{1,0:T(8,128)(2,1)}) %all-gather.11.cloned.1.call-update) | async-done | bytes 4194320 | tf_op jit(solution)/shard_map/all_gather | solution.py:61
  162.3 0.0 copy-start
  162.3 4.2 convolution_bitcast_fusion
  166.6 0.0 copy-done
  166.6 1.3 convolution_bitcast_fusion.1
  167.9 33.2 %all-gather.7.cloned.1.call-done = bf16[256,8192]{1,0:T(8,128)(2,1)} async-done(((bf16[256,512]{1,0:T(8,128)(2,1)}), bf16[256,8192]{1,0:T(8,128)(2,1)}) %all-gather.7.cloned.1.call-update) | async-done | bytes 4194320 | tf_op jit(solution)/shard_map/all_gather | solution.py:62
  201.1 0.0 copy-start.2
  201.1 4.2 multiply_convert_fusion.1
  205.4 0.0 copy-done.2
  205.4 1.3 fusion.7
  206.6 4.5 convolution_add_fusion
  211.1 0.0 reduce-scatter.3.cloned.1.call-update
  211.2 0.2 reduce-scatter.5.cloned.1.call-start
  211.4 0.0 copy-start.1
  211.4 3.3 fusion.1
  214.7 0.2 copy-done.1
  214.8 0.0 copy-start.3
  214.8 0.9 fusion.2
  215.8 1.3 copy-done.3
  217.0 1.0 fusion
  218.0 5.0 %pad_maximum_fusion = f32[8192,384]{0,1:T(8,128)} fusion(f32[8192,128]{0,1:T(8,128)S(1)} %fusion, f32[8192,128]{0,1:T(8,128)S(1)} %fusion.1, f32[8192,128]{0,1:T(8,128)S(1)} %fusion.2), kind=kLoop, calls=%fused_computation | loop fusion | flops 6291456 | bytes 25165824 | tf_op jit(solution)/shard_map/concatenate | solution.py:98
  223.0 0.0 reduce-scatter.5.cloned.1.call-update
  223.0 63.3 %reduce-scatter.3.cloned.1.call-done = f32[512,256]{1,0:T(8,128)} async-done(((f32[8192,256]{1,0:T(8,128)}), f32[512,256]{1,0:T(8,128)}) %reduce-scatter.3.cloned.1.call-update) | async-done | bytes 524304 | tf_op jit(solution)/shard_map/reduce_scatter | solution.py:48
  286.3 1.1 convert_bitcast_fusion
  287.4 0.8 copy.31
  288.2 151.6 %reduce-scatter.5.cloned.1.call-done = f32[1024,384]{0,1:T(8,128)} async-done(((f32[8192,384]{0,1:T(8,128)}), f32[1024,384]{0,1:T(8,128)}) %reduce-scatter.5.cloned.1.call-update) | async-done | bytes 1572880 | tf_op jit(solution)/shard_map/reduce_scatter | solution.py:48
  439.8 2.3 slice_bitcast_fusion
  442.1 1.0 copy.32
  443.1 1.0 copy.33
Async XLA Ops:
  7.2 44.0 %all-gather.9.cloned.1.call-start = ((), (), s32[]{:S(2)}) async-start(), calls=%async_computation.3 | async-start | bytes 2621440 | tf_op jit(solution)/shard_map/all_gather | solution.py:30
  20.2 105.7 %all-gather.13.cloned.1.call-start = ((), (), s32[]{:S(2)}) async-start(), calls=%async_computation.7 | async-start | bytes 4718592 | tf_op jit(solution)/shard_map/all_gather | solution.py:19
  22.1 140.2 %all-gather.11.cloned.1.call-start = ((), (), s32[]{:S(2)}) async-start(), calls=%async_computation.4 | async-start | bytes 4456448 | tf_op jit(solution)/shard_map/all_gather | solution.py:61
  22.8 178.3 %all-gather.7.cloned.1.call-start = ((), (), s32[]{:S(2)}) async-start(), calls=%async_computation.2 | async-start | bytes 4456448 | tf_op jit(solution)/shard_map/all_gather | solution.py:62
  23.4 262.9 %reduce-scatter.3.cloned.1.call-start = ((), (), s32[]{:S(2)}) async-start(), calls=%async_computation.5 | async-start | bytes 8912896 | tf_op jit(solution)/shard_map/reduce_scatter | solution.py:48
  162.3 4.2 copy-start
  201.1 4.3 copy-start.2
  211.2 228.6 %reduce-scatter.5.cloned.1.call-start = ((), (), s32[]{:S(2)}) async-start(), calls=%async_computation.6 | async-start | bytes 14155776 | tf_op jit(solution)/shard_map/reduce_scatter | solution.py:48
  211.4 3.5 copy-start.1
  214.8 2.2 copy-start.3
Sparse Core Ops, SparseCore 0:
  20.3 30.8 all-gather.8
  54.1 71.6 all-gather.12
  127.5 34.7 all-gather.10
  163.9 37.2 all-gather.6
  211.3 75.0 reduce-scatter.2
  290.1 149.6 reduce-scatter.4
where the time goes:
time: 451 us
  waiting for transfers between devices  369 us (82%)
  local copies, waits for them, and re-layouts  25.4 us (6%)
  matrix products  20.7 us (5%)
  between operations  14.2 us (3%)
  blocking collectives  12.9 us (3%)
  other arithmetic  7.91 us (2%)
    reduce_scatter x2, waiting for transfers between devices, own_rows(): lax.psum_scatter(portion(jnp.int32(0), count), axis, scatter_dimension=0,...  215 us
    all_gather x1, waiting for transfers between devices, one_gather(): lines, at, outs = (lax.all_gather(line, axis), 0, [])  70.3 us
    all_gather x1, waiting for transfers between devices, shards(): grads = lax.all_gather(out_grad, 'tp', axis=1, tiled=True)  33.2 us
    all_gather x1, waiting for transfers between devices, stacked_from(): parts = lax.all_gather(parts, axes[k], axis=0, tiled=True)  27.7 us
    all_gather x1, waiting for transfers between devices, shards(): whole = lax.all_gather(tokens, 'tp', axis=1, tiled=True)  21.9 us
    all_gather x1, blocking collectives, stacked_from(): parts = lax.all_gather(parts, axes[k], axis=0, tiled=True)  12.9 us
  transfers between devices with their start and end apart: 6, of which 6 were waited for; matrix products, arithmetic and copies ran while one was open for 9% of the time, Pallas kernels for 0%

commit v1 on v0

--- a/solution.py
+++ b/solution.py
@@ -27,7 +27,9 @@
 def stacked_from(value, axes, turns):
     parts = value[None]
     for k in turns:
-        parts = lax.all_gather(parts, axes[k], axis=0, tiled=True)
+        parts = jnp.concatenate(
+            lax.all_to_all(jnp.stack([parts] * lax.axis_size(axes[k])), axes[k], 0, 0), axis=0
+        )
     current = [lax.axis_size(axes[k]) for k in reversed(turns)]
     parts = parts.reshape(*current, *value.shape)
     turned = sorted(range(len(turns)), key=lambda place: turns[len(turns) - 1 - place])

time: 451 us -> 414 us (0.918)
  waiting for transfers between devices: 369 us -> 321 us
    all_gather x1, waiting for transfers between devices: 70.3 us -> 14.1 us  [one_gather(): lines, at, outs = (lax.all_gather(line, axis), 0, [])]
    all_to_all x0 -> x1, waiting for transfers between devices: none -> 36 us  [stacked_from(): lax.all_to_all(jnp.stack([parts] * lax.axis_size(axes[k])), axes[k], 0, 0)]
    all_gather x1 -> x0, waiting for transfers between devices: 27.7 us -> none  [stacked_from(): parts = lax.all_gather(parts, axes[k], axis=0, tiled=True)]
    all_to_all x0 -> x1, blocking collectives: none -> 14.5 us  [stacked_from(): lax.all_to_all(jnp.stack([parts] * lax.axis_size(axes[k])), axes[k], 0, 0)]
    all_gather x1 -> x0, blocking collectives: 12.9 us -> none  [stacked_from(): parts = lax.all_gather(parts, axes[k], axis=0, tiled=True)]
  transfers between devices with their start and end apart: 6 -> 6, of which waited for: 6 -> 6; matrix products, arithmetic and copies ran while one was open for 9% -> 10% of each run, Pallas kernels for 0% -> 0%
where the time goes in v1:
time: 414 us; the launch traced here: 413 us
  waiting for transfers between devices  321 us (78%)
  local copies, waits for them, and re-layouts  28.4 us (7%)
  matrix products  21.2 us (5%)
  blocking collectives  14.5 us (4%)
  between operations  13.8 us (3%)
  other arithmetic  8.95 us (2%)
  starting transfers between devices  4.81 us (1%)
    reduce_scatter x2, waiting for transfers between devices, own_rows(): lax.psum_scatter(portion(jnp.int32(0), count), axis, scatter_dimension=0,...  215 us
    all_to_all x1, waiting for transfers between devices, stacked_from(): lax.all_to_all(jnp.stack([parts] * lax.axis_size(axes[k])), axes[k], 0, 0)  36 us
    all_gather x1, waiting for transfers between devices, shards(): grads = lax.all_gather(out_grad, 'tp', axis=1, tiled=True)  32.9 us
    all_gather x1, waiting for transfers between devices, shards(): whole = lax.all_gather(tokens, 'tp', axis=1, tiled=True)  21.9 us
    all_to_all x1, blocking collectives, stacked_from(): lax.all_to_all(jnp.stack([parts] * lax.axis_size(axes[k])), axes[k], 0, 0)  14.5 us
    all_gather x1, waiting for transfers between devices, one_gather(): lines, at, outs = (lax.all_gather(line, axis), 0, [])  14.1 us
  transfers between devices with their start and end apart: 6, of which 6 were waited for; matrix products, arithmetic and copies ran while one was open for 10% of the time, Pallas kernels for 0%

profile of v1, /device:TPU:0, one launch (start us, length us, event | category | flops | bytes accessed | tf_op | source)
XLA Modules:
  0.0 413.1 jit_solution(3716258025490850368)
XLA Ops:
  7.2 0.0 all-gather.9.cloned.1.call-start
  7.2 1.9 pad_maximum_fusion.1
  9.1 0.0 all-gather.9.cloned.1.call-update
  9.1 0.0 all-gather.7.cloned.1.call-start
  9.1 0.7 all-gather.7.cloned.1.call-update
  9.8 1.1 pad_maximum_fusion.2
  10.9 14.5 %all_to_all.10 = bf16[2,1,128,1024]{3,2,1,0:T(8,128)(2,1)S(1)} all-to-all(bf16[2,1,128,1024]{3,2,1,0:T(8,128)(2,1)S(1)} %pad_maximum_fusion.2), channel_id=1, replica_groups=mesh['fsdp_0'=2,'fsdp_1'=4,'tp'=16] {'fsdp_0'}, dimensions={0} | all-to-all | bytes 1048576 | tf_op jit(solution)/shard_map/all_to_all | solution.py:31
  25.5 1.6 stack.7
  27.1 4.5 %all-to-all-start.1 = ((bf16[4,2,128,1024]{3,2,1,0:T(8,128)(2,1)}), bf16[4,2,128,1024]{3,2,1,0:T(8,128)(2,1)S(1)}, u32[]{:S(2)}, u32[]{:S(2)}) async-start(bf16[4,2,128,1024]{3,2,1,0:T(8,128)(2,1)} %stack.7), calls=%async_computation.1 | async-start | bytes 4194304 | tf_op jit(solution)/shard_map/all_to_all | solution.py:31
  31.5 0.0 all-gather.5.cloned.1.call-start
  31.5 0.7 all-gather.5.cloned.1.call-update
  32.3 0.0 reduce-scatter.3.cloned.1.call-start
  32.3 36.0 %all-to-all-done.1 = bf16[4,2,128,1024]{3,2,1,0:T(8,128)(2,1)S(1)} async-done(((bf16[4,2,128,1024]{3,2,1,0:T(8,128)(2,1)}), bf16[4,2,128,1024]{3,2,1,0:T(8,128)(2,1)S(1)}, u32[]{:S(2)}, u32[]{:S(2)}) %all-to-all-start.1) | async-done | bytes 2097184 | tf_op jit(solution)/shard_map/all_to_all | solution.py:31
  68.3 1.6 copy.16
  69.9 3.9 copy.17
  73.9 14.1 %all-gather.9.cloned.1.call-done = bf16[2097152]{0:T(1024)(128)(2,1)} async-done(((bf16[262144]{0:T(1024)(128)(2,1)}), bf16[2097152]{0:T(1024)(128)(2,1)}) %all-gather.9.cloned.1.call-update) | async-done | bytes 4194320 | tf_op jit(solution)/shard_map/all_gather | solution.py:19
  88.0 5.9 %reshape.26 = bf16[8,262144]{1,0:T(8,128)(2,1)} reshape(bf16[2097152]{0:T(1024)(128)(2,1)} %all-gather.9.cloned.1.call-done) | data formatting | bytes 8388608 | tf_op jit(solution)/shard_map/all_gather | solution.py:19
  93.8 3.9 fusion.6
  97.7 2.3 reshape_reshape.6
  100.0 2.6 reshape_reshape.7
  102.6 21.9 %all-gather.7.cloned.1.call-done = bf16[256,8192]{1,0:T(8,128)(2,1)} async-done(((bf16[256,512]{1,0:T(8,128)(2,1)}), bf16[256,8192]{1,0:T(8,128)(2,1)}) %all-gather.7.cloned.1.call-update) | async-done | bytes 4194320 | tf_op jit(solution)/shard_map/all_gather | solution.py:63
  124.5 0.0 copy-start
  124.5 4.5 %convolution_bitcast_fusion = f32[256,128]{0,1:T(8,128)S(1)} fusion(bf16[8192,128]{1,0:T(8,128)(2,1)} %reshape_reshape.6, bf16[256,8192]{1,0:T(8,128)(2,1)} %all-gather.7.cloned.1.call-done), kind=kOutput, calls=%fused_computation.8 | convolution fusion | flops 536870912 | bytes 6422528 | tf_op jit(solution)/shard_map/dot_general | solution.py:66
  128.9 0.0 copy-done
  128.9 1.6 convolution_bitcast_fusion.1
  130.5 32.9 %all-gather.5.cloned.1.call-done = bf16[256,8192]{1,0:T(8,128)(2,1)} async-done(((bf16[256,512]{1,0:T(8,128)(2,1)}), bf16[256,8192]{1,0:T(8,128)(2,1)}) %all-gather.5.cloned.1.call-update) | async-done | bytes 4194320 | tf_op jit(solution)/shard_map/all_gather | solution.py:64
  163.4 0.0 copy-start.2
  163.4 4.5 %multiply_convert_fusion.1 = (bf16[256,128]{0,1:T(8,128)(2,1)S(1)}, bf16[256,128]{0,1:T(8,128)(2,1)S(1)}) fusion(f32[256,128]{0,1:T(8,128)S(1)} %convolution_bitcast_fusion, f32[256,128]{0,1:T(8,128)S(1)} %convolution_bitcast_fusion.1, bf16[128,8192]{0,1:T(8,128)(2,1)} %bitcast.41, bf16[256,8192]{1,0:T(8,128)(2,1)} %all-gather.5.cloned.1.call-done), kind=kOutput, calls=%fused_computation.16 | convolution fusion | flops 537296896 | bytes 6684672 | tf_op jit(solution)/shard_map/dot_general | solution.py:71
  167.9 0.0 copy-done.2
  167.9 1.2 fusion.7
  169.2 4.5 %convolution_add_fusion = f32[8192,256]{1,0:T(8,128)} fusion(f32[8192,256]{1,0:T(8,128)S(1)} %fusion.7, bf16[8192,128]{1,0:T(8,128)(2,1)S(1)} %reshape_reshape.7, bf16[256,128]{0,1:T(8,128)(2,1)S(1)} %get-tuple-element.21), kind=kOutput, calls=%fused_computation.1 | convolution fusion | flops 538968064 | bytes 18939904 | tf_op jit(solution)/shard_map/dot_general | solution.py:90
  173.6 0.0 reduce-scatter.3.cloned.1.call-update
  173.6 0.2 reduce-scatter.5.cloned.1.call-start
  173.9 0.0 copy-start.1
  173.9 3.2 fusion.1
  177.1 0.2 copy-done.1
  177.3 0.0 copy-start.3
  177.3 0.9 fusion.2
  178.2 1.3 copy-done.3
  179.5 0.9 fusion
  180.4 4.9 %pad_maximum_fusion = f32[8192,384]{0,1:T(8,128)} fusion(f32[8192,128]{0,1:T(8,128)S(1)} %fusion, f32[8192,128]{0,1:T(8,128)S(1)} %fusion.1, f32[8192,128]{0,1:T(8,128)S(1)} %fusion.2), kind=kLoop, calls=%fused_computation | loop fusion | flops 6291456 | bytes 25165824 | tf_op jit(solution)/shard_map/concatenate | solution.py:100
  185.4 0.0 reduce-scatter.5.cloned.1.call-update
  185.4 63.4 %reduce-scatter.3.cloned.1.call-done = f32[512,256]{1,0:T(8,128)} async-done(((f32[8192,256]{1,0:T(8,128)}), f32[512,256]{1,0:T(8,128)}) %reduce-scatter.3.cloned.1.call-update) | async-done | bytes 524304 | tf_op jit(solution)/shard_map/reduce_scatter | solution.py:50
  248.8 1.1 convert_bitcast_fusion
  249.9 0.8 copy.18
  250.7 151.6 %reduce-scatter.5.cloned.1.call-done = f32[1024,384]{0,1:T(8,128)} async-done(((f32[8192,384]{0,1:T(8,128)}), f32[1024,384]{0,1:T(8,128)}) %reduce-scatter.5.cloned.1.call-update) | async-done | bytes 1572880 | tf_op jit(solution)/shard_map/reduce_scatter | solution.py:50
  402.3 2.3 slice_bitcast_fusion
  404.6 1.0 copy.19
  405.5 1.0 copy.20
Async XLA Ops:
  7.2 80.8 %all-gather.9.cloned.1.call-start = ((), (), s32[]{:S(2)}) async-start(), calls=%async_computation.8 | async-start | bytes 4718592 | tf_op jit(solution)/shard_map/all_gather | solution.py:19
  9.1 115.4 %all-gather.7.cloned.1.call-start = ((), (), s32[]{:S(2)}) async-start(), calls=%async_computation.5 | async-start | bytes 4456448 | tf_op jit(solution)/shard_map/all_gather | solution.py:63
  27.1 41.2 %all-to-all-start.1 = ((bf16[4,2,128,1024]{3,2,1,0:T(8,128)(2,1)}), bf16[4,2,128,1024]{3,2,1,0:T(8,128)(2,1)S(1)}, u32[]{:S(2)}, u32[]{:S(2)}) async-start(bf16[4,2,128,1024]{3,2,1,0:T(8,128)(2,1)} %stack.7), calls=%async_computation.1 | async-start | bytes 4194304 | tf_op jit(solution)/shard_map/all_to_all | solution.py:31
  31.5 131.9 %all-gather.5.cloned.1.call-start = ((), (), s32[]{:S(2)}) async-start(), calls=%async_computation.4 | async-start | bytes 4456448 | tf_op jit(solution)/shard_map/all_gather | solution.py:64
  32.3 216.5 %reduce-scatter.3.cloned.1.call-start = ((), (), s32[]{:S(2)}) async-start(), calls=%async_computation.6 | async-start | bytes 8912896 | tf_op jit(solution)/shard_map/reduce_scatter | solution.py:50
  124.5 4.5 %copy-start = (bf16[256,8192]{1,0:T(8,128)(2,1)S(1)}, bf16[256,8192]{1,0:T(8,128)(2,1)}, u32[]{:S(2)}) copy-start(bf16[256,8192]{1,0:T(8,128)(2,1)} %all-gather.7.cloned.1.call-done) | copy-start | bytes 12582916
  163.4 4.5 %copy-start.2 = (bf16[8192,128]{1,0:T(8,128)(2,1)S(1)}, bf16[8192,128]{1,0:T(8,128)(2,1)}, u32[]{:S(2)}) copy-start(bf16[8192,128]{1,0:T(8,128)(2,1)} %reshape_reshape.6) | copy-start | bytes 6291460
  173.6 228.6 %reduce-scatter.5.cloned.1.call-start = ((), (), s32[]{:S(2)}) async-start(), calls=%async_computation.7 | async-start | bytes 14155776 | tf_op jit(solution)/shard_map/reduce_scatter | solution.py:50
  173.9 3.5 copy-start.1
  177.3 2.2 copy-start.3
Sparse Core Ops, SparseCore 0:
  10.9 77.0 all-gather.8
  89.6 34.7 all-gather.6
  126.1 37.2 all-gather.4
  173.8 75.0 reduce-scatter.2
  252.6 149.6 reduce-scatter.4
